TPU v7x, 32 devices: a whole 2x2x4 slice. The times are simulated.
32 devices in a mesh: prow: 4 (over z), pcol: 8 (over y, x, core).
Axes of the slice: x: 2, y: 2, z: 4, core: 2. Of those that a mesh axis runs over, the one named last changes fastest.
Arguments:
- points: float32 [1, 8, 2, 1024], P(None, 'pcol'), may hold values from 0 to 1
- range_length: float32 [1], replicated, may hold values from 0.05 to 0.15
- smoothness: int32 [1], replicated, may hold values from 0 to 2
- sketch_bank: bfloat16 [8, 48, 1024], P('pcol'), may hold values from -6 to 6
- sketch_ids: int32 [2, 4, 1, 8], P(None, 'prow', None, 'pcol'), may hold values from 0 to 7
- tile_ranks: int32 [2, 4, 1, 8], P(None, 'prow', None, 'pcol'), may hold values from 16 to 48
Outputs:
- y_factors: float32 [2, 4, 1, 8, 48, 1024], P(None, 'prow', None, 'pcol')
- c_factors: float32 [2, 4, 1, 8, 48, 1024], P(None, 'prow', None, 'pcol')
- tile_error: float32 [2, 4, 1, 8], P(None, 'prow', None, 'pcol')
- rank_total: int32 [1], replicated
All inputs are finite; a program needn't handle non-finite values.
Results may differ from a plain program's by a relative error of at most 0.0098.
The roundings to bfloat16 on the way count: a program that leaves them out, or rounds other values in their place, can miss the bound.
Values may be sent and summed in bfloat16 or wider, within the bound.
A program may use at most 64 MiB of HBM per device.

v0:
```python
import jax
import jax.numpy as jnp
from jax import lax
from jax.sharding import PartitionSpec as P


def kernel_factors(smoothness, range_length):
    morton_value = smoothness[0].astype(jnp.float32)
    kernel_scale = jnp.sqrt(2.0 * morton_value + 1.0) / range_length[0]
    linear_factor = jnp.where(smoothness[0] >= 1, 1.0, 0.0).astype(jnp.float32)
    squared_distance = jnp.where(smoothness[0] >= 2, 1.0 / 3.0, 0.0).astype(jnp.float32)
    return (kernel_scale, linear_factor, squared_distance)


def covariance_tile(row_locations, column_locations, kernel_scale, linear_factor, squared_distance):
    offset_horizontal = row_locations[0][:, None] - column_locations[0][None, :]
    offset_vertical = row_locations[1][:, None] - column_locations[1][None, :]
    scaled_distance = kernel_scale * jnp.sqrt(
        offset_horizontal * offset_horizontal + offset_vertical * offset_vertical
    )
    return (
        1.0 + linear_factor * scaled_distance + squared_distance * scaled_distance * scaled_distance
    ) * jnp.exp(-scaled_distance)


def compress(tile_low, sketch, rank):
    keep = jnp.arange(sketch.shape[0]) < rank
    sketch = jnp.where(keep[:, None], sketch, jnp.zeros_like(sketch))
    sketched = lax.dot_general(
        sketch, tile_low, (((1,), (1,)), ((), ())), preferred_element_type=jnp.float32
    )
    product = jnp.dot(sketched.astype(jnp.bfloat16), tile_low, preferred_element_type=jnp.float32)
    gram = jnp.dot(sketched, sketched.T, precision=lax.Precision.HIGHEST)
    shift = 0.1 * jnp.trace(gram) / rank.astype(jnp.float32)
    gram = gram + jnp.diag(jnp.where(keep, shift, jnp.ones_like(shift)))
    factor = jnp.linalg.cholesky(gram)
    coeffs = jax.scipy.linalg.cho_solve((factor, True), product)
    approx = lax.dot_general(
        sketched, coeffs, (((0,), (0,)), ((), ())), precision=lax.Precision.HIGHEST
    )
    error = tile_low.astype(jnp.float32) - approx
    return (sketched, coeffs, jnp.sum(error * error))


def per_device(points, range_length, smoothness, sketch_bank, sketch_ids, tile_ranks):
    row_count = lax.axis_size("prow")
    col_count = lax.axis_size("pcol")
    row_place = lax.axis_index("prow")
    col_place = lax.axis_index("pcol")
    row_tiles = sketch_ids.shape[0]
    col_tiles = sketch_ids.shape[2]
    tile_size = points.shape[3]
    sketch_rows = sketch_bank.shape[1]
    slots_total = row_tiles * col_tiles
    tiles_across = col_tiles * col_count
    kernel_scale, linear_factor, squared_distance = kernel_factors(smoothness, range_length)
    gathered = lax.all_gather(points, "pcol", axis=1, tiled=True)
    every_block = gathered.reshape(tiles_across, 2, tile_size)
    row_index = jnp.arange(row_tiles, dtype=jnp.int32) * row_count + row_place
    col_index = jnp.arange(col_tiles, dtype=jnp.int32) * col_count + col_place
    slot_row = jnp.repeat(row_index, col_tiles)
    slot_col = jnp.tile(col_index, row_tiles)
    own_ids = sketch_ids.reshape(slots_total)
    own_ranks = tile_ranks.reshape(slots_total)
    lower = slot_col <= slot_row
    offdiag = slot_col < slot_row
    ranks_local = jnp.sum(jnp.where(offdiag, own_ranks, 0))
    rank_sum = lax.psum(ranks_local, ("prow", "pcol"))
    bank_whole = lax.all_gather(sketch_bank, "pcol", axis=0, tiled=True)
    chosen = bank_whole[own_ids]
    row_points_all = every_block[slot_row]
    col_points_all = every_block[slot_col]

    def one_tile(row_locations, column_locations, sketch, rank):
        tile_block = covariance_tile(
            row_locations, column_locations, kernel_scale, linear_factor, squared_distance
        )
        norm_sq = jnp.sum(tile_block * tile_block)
        sketched, coeffs, err_sq = compress(tile_block.astype(jnp.bfloat16), sketch, rank)
        return (sketched, coeffs, norm_sq, err_sq)

    def mapped(inputs):
        return one_tile(inputs[0], inputs[1], inputs[2], inputs[3])

    sketched_all, coeffs_all, norm_all, err_all = lax.map(
        mapped, (row_points_all, col_points_all, chosen, own_ranks)
    )
    norm_local = jnp.sum(jnp.where(lower, jnp.where(offdiag, 2.0, 1.0) * norm_all, 0.0))
    total = lax.psum(norm_local, ("prow", "pcol"))
    errors = (
        jnp.where(offdiag, jnp.sqrt(err_all), jnp.sqrt(norm_all)) * tiles_across / jnp.sqrt(total)
    )
    errors = jnp.where(lower, errors, 0.0)
    out_shape = (row_tiles, 1, col_tiles, 1, sketch_rows, tile_size)
    y_out = jnp.where(offdiag[:, None, None], sketched_all, 0.0).reshape(out_shape)
    c_out = jnp.where(offdiag[:, None, None], coeffs_all, 0.0).reshape(out_shape)
    err_out = errors.reshape(row_tiles, 1, col_tiles, 1)
    rank_out = rank_sum.reshape(1)
    return (y_out, c_out, err_out, rank_out)


def solution(mesh):
    in_specs = (
        P(None, "pcol", None, None),
        P(),
        P(),
        P("pcol", None, None),
        P(None, "prow", None, "pcol"),
        P(None, "prow", None, "pcol"),
    )
    out_specs = (
        P(None, "prow", None, "pcol", None, None),
        P(None, "prow", None, "pcol", None, None),
        P(None, "prow", None, "pcol"),
        P(),
    )
    return jax.shard_map(
        per_device, mesh=mesh, in_specs=in_specs, out_specs=out_specs, check_vma=False
    )
```

profile of v0, /device:TPU:0, one launch (start us, length us, event | category | flops | bytes accessed | tf_op | source)
XLA Modules:
  0.0 177.8 jit_solution(8479940237843029648)
XLA Ops:
  0.6 0.0 copy-start.1
  0.7 10.9 %all_gather.7 = f32[1,8,2,1024]{3,2,0,1:T(2,128)S(1)} all-gather(f32[1,1,2,1024]{3,2,0,1:T(2,128)} %bitcast.135), channel_id=1, replica_groups=mesh['prow'=4,'pcol'=8] {'pcol'}, dimensions={1}, use_global_device_ids=true | all-gather | bytes 73728 | tf_op jit(solution)/shard_map/all_gather | solution.py:57
  11.6 0.6 gather_fusion.2
  12.2 0.6 gather_fusion.1
  14.1 10.2 %all_gather.6 = bf16[8,48,1024]{2,1,0:T(8,128)(2,1)S(1)} all-gather(bf16[1,48,1024]{2,1,0:T(8,128)(2,1)} %param.11), channel_id=1, replica_groups=mesh['prow'=4,'pcol'=8] {'pcol'}, dimensions={0}, use_global_device_ids=true | all-gather | bytes 884736 | tf_op jit(solution)/shard_map/all_gather | solution.py:69
  24.4 0.0 copy-done.1
  24.4 0.0 copy-start
  24.4 0.6 gather_fusion
  25.0 0.0 copy-done
  25.0 68.5 %while.17 = (s32[]{:T(128)}, f32[2,48,1024]{2,1,0:T(8,128)S(1)}, f32[2,48,1024]{2,1,0:T(8,128)S(1)}, f32[2]{0:T(128)S(1)}, f32[2]{0:T(128)S(1)}, /*index=5*/s32[...) while((s32[]{:T(128)}, f32[2,48,1024]{2,1,0:T(8,128)S(1)}, ...), condition=%wide.region_6.7_spmd.clone, body=%wide.region_0.6_spmd.sunk.clone | while | flops 954344128 | bytes 2676799 | solution.py:85
  25.1 0.7 dynamic_slice.26
  25.8 0.7 iota_compare_fusion.6
  26.5 3.2 %bitcast_dynamic-update-slice_fusion.6 = (f32[2,48,1024]{2,1,0:T(8,128)S(1)}, f32[48,1024]{1,0:T(8,128)S(1)}) fusion(f32[2,48,1024]{2,1,0:T(8,128)S(1)} %get-tuple-element.256, s32[]{:T(128)} %get-tuple-element.255, f32[]{:T(128)} %get-tuple-element.278, f32[1024]{0:T(1024)S(1)} %bitcast.123, f32[1024]{0:T(1024)S(1)} %bitcast.127, ...), kind=kOutput, calls=%fused_computation.12.clone.1.clone | convolution fusion | flops 115392512 | bytes 510976 | tf_op jit(solution)/shard_map/while/body/eval_jaxpr/dot_general | solution.py:29
  29.6 0.9 select_reduce_fusion.7
  30.5 0.1 copy.15
  31.9 0.7 broadcast_select_fusion.3
  32.6 0.1 fusion.68
  32.7 4.4 %cholesky.73 = f32[48,48]{1,0:T(8,128)S(1)} custom-call(f32[48,48]{1,0:T(8,128)S(1)} %fusion.68), custom_call_target="Cholesky" | custom-call | tf_op jit(solution)/shard_map/while/body/eval_jaxpr/jit(cholesky)/cholesky | solution.py:36
  37.1 0.7 compare_reduce_fusion.3
  37.8 0.7 fusion.69
  38.5 3.7 %custom-call.20 = f32[1,48,48]{1,2,0:T(8,128)S(1)} custom-call(f32[1,48,48]{2,1,0:T(8,128)S(1)} %fusion.69), custom_call_target="InvertDiagBlocksLowerTriangular" | custom-call | tf_op jit(solution)/shard_map/while/body/eval_jaxpr/jit(_cho_solve)/triangular_solve | solution.py:37
  42.2 3.2 %fusion.67 = f32[48,1024]{1,0:T(8,128)S(1)} fusion(f32[]{:T(128)} %get-tuple-element.278, f32[1024]{0:T(1024)S(1)} %bitcast.124, f32[1024]{0:T(1024)S(1)} %bitcast.128, f32[1024]{0:T(1024)S(1)} %bitcast.120, f32[1024]{0:T(1024)S(1)} %bitcast.132, f32[]{:T(128)} %get-tuple-element.275, f32[]{:T(128)} %get-tuple-element.274, ...), kind=kOutput, calls=%fused_computation.9.clone.1.clone | convolution fusion | flops 115392512 | bytes 409612 | tf_op jit(solution)/shard_map/while/body/eval_jaxpr/dot_general | solution.py:32
  45.4 0.4 fusion.70
  45.7 0.3 bitcast_dynamic-update-slice_fusion.7
  46.1 7.4 %multiply_reduce_fusion.7 = f32[]{:T(128)} fusion(f32[48,1024]{1,0:T(8,128)S(1)} %get-tuple-element.222, f32[48,1024]{1,0:T(8,128)S(1)} %get-tuple-element.226, f32[]{:T(128)} %get-tuple-element.278, f32[1024]{0:T(1024)S(1)} %bitcast.125, f32[1024]{0:T(1024)S(1)} %bitcast.129, f32[1024]{0:T(1024)S(1)} %bitcast.121, f32[1024]{0:T(1024)S(1)} %bitcast.133, ...), kind=kOutput, calls=%fused_computation.6.clone.1.clone | convolution fusion | flops 622854144 | bytes 409616 | tf_op jit(solution)/shard_map/while/body/eval_jaxpr/dot_general | solution.py:38
  53.5 0.8 dynamic_update_slice.27
  54.3 4.2 %multiply_reduce_fusion.6 = f32[]{:T(128)} fusion(f32[]{:T(128)} %get-tuple-element.278, f32[1024]{0:T(1024)S(1)} %bitcast.126, f32[1024]{0:T(1024)S(1)} %bitcast.130, f32[1024]{0:T(1024)S(1)} %bitcast.122, f32[1024]{0:T(1024)S(1)} %bitcast.134, f32[]{:T(128)} %get-tuple-element.275, f32[]{:T(128)} %get-tuple-element.274), kind=kLoop, calls=%fused_computation.7.clone.1.clone | loop fusion | flops 15728639 | bytes 16400 | tf_op jit(solution)/shard_map/while/body/eval_jaxpr/reduce_sum | solution.py:78
  58.5 0.8 dynamic_update_slice.26
  59.4 0.7 dynamic_slice.26
  60.0 0.7 iota_compare_fusion.6
  60.7 3.2 %bitcast_dynamic-update-slice_fusion.6 = (f32[2,48,1024]{2,1,0:T(8,128)S(1)}, f32[48,1024]{1,0:T(8,128)S(1)}) fusion(f32[2,48,1024]{2,1,0:T(8,128)S(1)} %get-tuple-element.256, s32[]{:T(128)} %get-tuple-element.255, f32[]{:T(128)} %get-tuple-element.278, f32[1024]{0:T(1024)S(1)} %bitcast.123, f32[1024]{0:T(1024)S(1)} %bitcast.127, ...), kind=kOutput, calls=%fused_computation.12.clone.1.clone | convolution fusion | flops 115392512 | bytes 510976 | tf_op jit(solution)/shard_map/while/body/eval_jaxpr/dot_general | solution.py:29
  63.9 0.9 select_reduce_fusion.7
  64.8 0.1 copy.15
  66.2 0.7 broadcast_select_fusion.3
  66.9 0.1 fusion.68
  66.9 4.4 %cholesky.73 = f32[48,48]{1,0:T(8,128)S(1)} custom-call(f32[48,48]{1,0:T(8,128)S(1)} %fusion.68), custom_call_target="Cholesky" | custom-call | tf_op jit(solution)/shard_map/while/body/eval_jaxpr/jit(cholesky)/cholesky | solution.py:36
  71.3 0.7 compare_reduce_fusion.3
  72.1 0.7 fusion.69
  72.8 3.7 %custom-call.20 = f32[1,48,48]{1,2,0:T(8,128)S(1)} custom-call(f32[1,48,48]{2,1,0:T(8,128)S(1)} %fusion.69), custom_call_target="InvertDiagBlocksLowerTriangular" | custom-call | tf_op jit(solution)/shard_map/while/body/eval_jaxpr/jit(_cho_solve)/triangular_solve | solution.py:37
  76.4 3.2 %fusion.67 = f32[48,1024]{1,0:T(8,128)S(1)} fusion(f32[]{:T(128)} %get-tuple-element.278, f32[1024]{0:T(1024)S(1)} %bitcast.124, f32[1024]{0:T(1024)S(1)} %bitcast.128, f32[1024]{0:T(1024)S(1)} %bitcast.120, f32[1024]{0:T(1024)S(1)} %bitcast.132, f32[]{:T(128)} %get-tuple-element.275, f32[]{:T(128)} %get-tuple-element.274, ...), kind=kOutput, calls=%fused_computation.9.clone.1.clone | convolution fusion | flops 115392512 | bytes 409612 | tf_op jit(solution)/shard_map/while/body/eval_jaxpr/dot_general | solution.py:32
  79.6 0.4 fusion.70
  80.0 0.3 bitcast_dynamic-update-slice_fusion.7
  80.3 7.4 %multiply_reduce_fusion.7 = f32[]{:T(128)} fusion(f32[48,1024]{1,0:T(8,128)S(1)} %get-tuple-element.222, f32[48,1024]{1,0:T(8,128)S(1)} %get-tuple-element.226, f32[]{:T(128)} %get-tuple-element.278, f32[1024]{0:T(1024)S(1)} %bitcast.125, f32[1024]{0:T(1024)S(1)} %bitcast.129, f32[1024]{0:T(1024)S(1)} %bitcast.121, f32[1024]{0:T(1024)S(1)} %bitcast.133, ...), kind=kOutput, calls=%fused_computation.6.clone.1.clone | convolution fusion | flops 622854144 | bytes 409616 | tf_op jit(solution)/shard_map/while/body/eval_jaxpr/dot_general | solution.py:38
  87.8 0.8 dynamic_update_slice.27
  88.6 4.2 %multiply_reduce_fusion.6 = f32[]{:T(128)} fusion(f32[]{:T(128)} %get-tuple-element.278, f32[1024]{0:T(1024)S(1)} %bitcast.126, f32[1024]{0:T(1024)S(1)} %bitcast.130, f32[1024]{0:T(1024)S(1)} %bitcast.122, f32[1024]{0:T(1024)S(1)} %bitcast.134, f32[]{:T(128)} %get-tuple-element.275, f32[]{:T(128)} %get-tuple-element.274), kind=kLoop, calls=%fused_computation.7.clone.1.clone | loop fusion | flops 15728639 | bytes 16400 | tf_op jit(solution)/shard_map/while/body/eval_jaxpr/reduce_sum | solution.py:78
  92.8 0.8 dynamic_update_slice.26
  93.6 0.6 fusion.22
  94.2 39.7 %psum.14 = f32[]{:T(128)} all-reduce(f32[]{:T(128)} %fusion.22), channel_id=1, replica_groups=mesh['prow'=4,'pcol'=8] {'prow','pcol'}, use_global_device_ids=true, to_apply=%region_8.9 | all-reduce | flops 1 | bytes 8 | tf_op jit(solution)/shard_map/psum | solution.py:89
  134.6 0.5 fusion.25
  135.1 1.0 select_bitcast_fusion
  136.2 0.6 select_reduce_fusion.2
  136.8 41.0 %psum.15 = s32[1]{0:T(128)} all-reduce(s32[1]{0:T(128)} %bitcast.25), channel_id=1, replica_groups=mesh['prow'=4,'pcol'=8] {'prow','pcol'}, use_global_device_ids=true, to_apply=%region_10.11 | all-reduce | flops 1 | bytes 8 | tf_op jit(solution)/shard_map/psum | solution.py:68
  (15 shorter events, 0.2 us)
Async XLA Ops:
  0.6 23.7 %copy-start.1 = (s32[2,1,1,1]{0,3,2,1:T(1,128)S(1)}, s32[2,1,1,1]{0,3,2,1:T(1,128)}, u32[]{:S(2)}) copy-start(s32[2,1,1,1]{0,3,2,1:T(1,128)} %param.12) | copy-start | bytes 28
  24.4 0.7 copy-start
where the time goes:
time: 178 us
  blocking collectives  102 us (57%)
  other arithmetic  33.2 us (19%)
  matrix products  30.7 us (17%)
  local copies, waits for them, and re-layouts  6.5 us (4%)
  between operations  2.82 us (2%)
  loops' own time  2.75 us (2%)
    psum x1, blocking collectives, per_device(): rank_sum = lax.psum(ranks_local, ('prow', 'pcol'))  41 us
    psum x1, blocking collectives, per_device(): total = lax.psum(norm_local, ('prow', 'pcol'))  39.7 us
    dot_general x2, matrix products, compress(): lax.dot_general(sketched, coeffs, (((0,), (0,)), ((), ())), precision=lax...  14.9 us
    all_gather x1, blocking collectives, per_device(): gathered = lax.all_gather(points, 'pcol', axis=1, tiled=True)  10.9 us
    another operation x6, other arithmetic, compress(): factor = jnp.linalg.cholesky(gram)  10.3 us
    all_gather x1, blocking collectives, per_device(): bank_whole = lax.all_gather(sketch_bank, 'pcol', axis=0, tiled=True)  10.2 us
    another operation x4, other arithmetic, compress(): coeffs = jax.scipy.linalg.cho_solve((factor, True), product)  8.74 us
    reduce_sum x2, other arithmetic, one_tile(): norm_sq = jnp.sum(tile_block * tile_block)  8.47 us

commit v1 on v0

--- a/solution.py
+++ b/solution.py
@@ -66,7 +66,12 @@
     offdiag = slot_col < slot_row
     ranks_local = jnp.sum(jnp.where(offdiag, own_ranks, 0))
     rank_sum = lax.psum(ranks_local, ("prow", "pcol"))
-    bank_whole = lax.all_gather(sketch_bank, "pcol", axis=0, tiled=True)
+    ring = [sketch_bank]
+    for hop in range(7):
+        ring.append(lax.ppermute(ring[-1], "pcol", [(dev, (dev + 1) % 8) for dev in range(8)]))
+    bank_whole = jnp.roll(
+        jnp.concatenate(ring[::-1], axis=0), (lax.axis_index("pcol") + 1) * ring[0].shape[0], axis=0
+    )
     chosen = bank_whole[own_ids]
     row_points_all = every_block[slot_row]
     col_points_all = every_block[slot_col]

time: 178 us -> 194 us (1.090)
  waiting for transfers between devices: 0 us -> 25.7 us
  blocking collectives: 102 us -> 91.1 us
    ppermute x0 -> x7, waiting for transfers between devices: none -> 25.7 us  [per_device(): lax.ppermute(ring[-1], 'pcol', [(dev, (dev + 1) % 8) for dev in range(8)])]
    all_gather x1 -> x0, blocking collectives: 10.2 us -> none  [per_device(): bank_whole = lax.all_gather(sketch_bank, 'pcol', axis=0, tiled=True)]
  transfers between devices with their start and end apart: 0 -> 7, of which waited for: 0 -> 6; matrix products, arithmetic and copies ran while one was open for 0% -> 2% of each run, Pallas kernels for 0% -> 0%
where the time goes in v1:
time: 194 us; the launch traced here: 193 us
  blocking collectives  91.1 us (47%)
  other arithmetic  33.5 us (17%)
  matrix products  30.5 us (16%)
  waiting for transfers between devices  25.7 us (13%)
  local copies, waits for them, and re-layouts  6.03 us (3%)
  between operations  2.93 us (2%)
  loops' own time  2.64 us (1%)
    psum x1, blocking collectives, per_device(): total = lax.psum(norm_local, ('prow', 'pcol'))  41.3 us
    psum x1, blocking collectives, per_device(): rank_sum = lax.psum(ranks_local, ('prow', 'pcol'))  39.8 us
    ppermute x7, waiting for transfers between devices, per_device(): lax.ppermute(ring[-1], 'pcol', [(dev, (dev + 1) % 8) for dev in range(8)])  25.7 us
    dot_general x2, matrix products, compress(): lax.dot_general(sketched, coeffs, (((0,), (0,)), ((), ())), precision=lax...  14.7 us
    another operation x6, other arithmetic, compress(): factor = jnp.linalg.cholesky(gram)  10.1 us
    all_gather x1, blocking collectives, per_device(): gathered = lax.all_gather(points, 'pcol', axis=1, tiled=True)  9.98 us
    another operation x4, other arithmetic, compress(): coeffs = jax.scipy.linalg.cho_solve((factor, True), product)  8.47 us
    reduce_sum x2, other arithmetic, one_tile(): norm_sq = jnp.sum(tile_block * tile_block)  8.3 us
  transfers between devices with their start and end apart: 7, of which 6 were waited for; matrix products, arithmetic and copies ran while one was open for 2% of the time, Pallas kernels for 0%

profile of v1, /device:TPU:0, one launch (start us, length us, event | category | flops | bytes accessed | tf_op | source)
XLA Modules:
  0.0 193.4 jit_solution(9845030584155538405)
XLA Ops:
  0.6 0.5 collective-permute-start
  1.2 5.4 %collective-permute-done = bf16[1,48,1024]{2,1,0:T(8,128)(2,1)S(1)} collective-permute-done((bf16[1,48,1024]{2,1,0:T(8,128)(2,1)}, bf16[1,48,1024]{2,1,0:T(8,128)(2,1)S(1)}, u32[]{:S(2)}, u32[]{:S(2)}) %collective-permute-start) | collective-permute-done | bytes 98336 | tf_op jit(solution)/shard_map/ppermute | solution.py:71
  6.6 0.0 collective-permute-start.1
  6.6 0.7 fusion.23
  7.2 10.0 %all_gather.3 = f32[1,8,2,1024]{3,2,0,1:T(2,128)S(1)} all-gather(f32[1,1,2,1024]{3,2,0,1:T(2,128)} %bitcast.135), channel_id=1, replica_groups=mesh['prow'=4,'pcol'=8] {'pcol'}, dimensions={1}, use_global_device_ids=true | all-gather | bytes 73728 | tf_op jit(solution)/shard_map/all_gather | solution.py:57
  17.2 0.0 collective-permute-done.1
  17.2 0.4 collective-permute-start.2
  17.6 0.6 gather_fusion.2
  18.2 4.0 %collective-permute-done.2 = bf16[1,48,1024]{2,1,0:T(8,128)(2,1)S(1)} collective-permute-done((bf16[1,48,1024]{2,1,0:T(8,128)(2,1)S(1)}, bf16[1,48,1024]{2,1,0:T(8,128)(2,1)S(1)}, u32[]{:S(2)}, u32[]{:S(2)}) %collective-permute-start.2) | collective-permute-done | bytes 98336 | tf_op jit(solution)/shard_map/ppermute | solution.py:71
  22.2 0.0 collective-permute-start.3
  22.2 4.9 %collective-permute-done.3 = bf16[1,48,1024]{2,1,0:T(8,128)(2,1)S(1)} collective-permute-done((bf16[1,48,1024]{2,1,0:T(8,128)(2,1)S(1)}, bf16[1,48,1024]{2,1,0:T(8,128)(2,1)S(1)}, u32[]{:S(2)}, u32[]{:S(2)}) %collective-permute-start.3) | collective-permute-done | bytes 98336 | tf_op jit(solution)/shard_map/ppermute | solution.py:71
  27.1 0.0 collective-permute-start.4
  27.1 0.6 gather_fusion.1
  29.1 3.0 %collective-permute-done.4 = bf16[1,48,1024]{2,1,0:T(8,128)(2,1)S(1)} collective-permute-done((bf16[1,48,1024]{2,1,0:T(8,128)(2,1)S(1)}, bf16[1,48,1024]{2,1,0:T(8,128)(2,1)S(1)}, u32[]{:S(2)}, u32[]{:S(2)}) %collective-permute-start.4) | collective-permute-done | bytes 98336 | tf_op jit(solution)/shard_map/ppermute | solution.py:71
  32.1 0.0 collective-permute-start.5
  32.1 1.4 select_reduce_fusion.2
  33.4 3.6 %collective-permute-done.5 = bf16[1,48,1024]{2,1,0:T(8,128)(2,1)S(1)} collective-permute-done((bf16[1,48,1024]{2,1,0:T(8,128)(2,1)S(1)}, bf16[1,48,1024]{2,1,0:T(8,128)(2,1)S(1)}, u32[]{:S(2)}, u32[]{:S(2)}) %collective-permute-start.5) | collective-permute-done | bytes 98336 | tf_op jit(solution)/shard_map/ppermute | solution.py:71
  37.0 0.0 collective-permute-start.6
  37.0 4.9 %collective-permute-done.6 = bf16[1,48,1024]{2,1,0:T(8,128)(2,1)S(1)} collective-permute-done((bf16[1,48,1024]{2,1,0:T(8,128)(2,1)S(1)}, bf16[1,48,1024]{2,1,0:T(8,128)(2,1)S(1)}, u32[]{:S(2)}, u32[]{:S(2)}) %collective-permute-start.6) | collective-permute-done | bytes 98336 | tf_op jit(solution)/shard_map/ppermute | solution.py:71
  42.2 0.0 copy-start.1
  42.2 0.1 constant_dynamic-slice_fusion.4
  42.3 0.6 gather_fusion
  43.0 66.5 %while.17 = (s32[]{:T(128)}, f32[2,48,1024]{2,1,0:T(8,128)S(1)}, f32[2,48,1024]{2,1,0:T(8,128)S(1)}, f32[2]{0:T(128)S(1)}, f32[2]{0:T(128)S(1)}, /*index=5*/s32[...) while((s32[]{:T(128)}, f32[2,48,1024]{2,1,0:T(8,128)S(1)}, ...), condition=%wide.region_6.7_spmd.clone, body=%wide.region_0.6_spmd.sunk.clone | while | flops 954344128 | bytes 2676799 | solution.py:90
  43.0 0.6 dynamic_slice.32
  43.6 0.6 iota_compare_fusion.6
  44.2 3.2 %bitcast_dynamic-update-slice_fusion.6 = (f32[2,48,1024]{2,1,0:T(8,128)S(1)}, f32[48,1024]{1,0:T(8,128)S(1)}) fusion(f32[2,48,1024]{2,1,0:T(8,128)S(1)} %get-tuple-element.258, s32[]{:T(128)} %get-tuple-element.257, f32[]{:T(128)} %get-tuple-element.280, f32[1024]{0:T(1024)S(1)} %bitcast.123, f32[1024]{0:T(1024)S(1)} %bitcast.127, ...), kind=kOutput, calls=%fused_computation.12.clone.1.clone | convolution fusion | flops 115392512 | bytes 510976 | tf_op jit(solution)/shard_map/while/body/eval_jaxpr/dot_general | solution.py:29
  47.3 0.9 select_reduce_fusion.7
  48.2 0.1 copy.15
  49.6 0.6 broadcast_select_fusion.3
  50.1 0.1 fusion.68
  50.2 4.4 %cholesky.73 = f32[48,48]{1,0:T(8,128)S(1)} custom-call(f32[48,48]{1,0:T(8,128)S(1)} %fusion.68), custom_call_target="Cholesky" | custom-call | tf_op jit(solution)/shard_map/while/body/eval_jaxpr/jit(cholesky)/cholesky | solution.py:36
  54.6 0.6 compare_reduce_fusion.3
  55.3 0.6 fusion.69
  55.8 3.7 %custom-call.22 = f32[1,48,48]{1,2,0:T(8,128)S(1)} custom-call(f32[1,48,48]{2,1,0:T(8,128)S(1)} %fusion.69), custom_call_target="InvertDiagBlocksLowerTriangular" | custom-call | tf_op jit(solution)/shard_map/while/body/eval_jaxpr/jit(_cho_solve)/triangular_solve | solution.py:37
  59.5 3.2 %fusion.67 = f32[48,1024]{1,0:T(8,128)S(1)} fusion(f32[]{:T(128)} %get-tuple-element.280, f32[1024]{0:T(1024)S(1)} %bitcast.124, f32[1024]{0:T(1024)S(1)} %bitcast.128, f32[1024]{0:T(1024)S(1)} %bitcast.120, f32[1024]{0:T(1024)S(1)} %bitcast.132, f32[]{:T(128)} %get-tuple-element.277, f32[]{:T(128)} %get-tuple-element.276, ...), kind=kOutput, calls=%fused_computation.9.clone.1.clone | convolution fusion | flops 115392512 | bytes 409612 | tf_op jit(solution)/shard_map/while/body/eval_jaxpr/dot_general | solution.py:32
  62.7 0.4 fusion.70
  63.1 0.3 bitcast_dynamic-update-slice_fusion.7
  63.4 7.3 %multiply_reduce_fusion.7 = f32[]{:T(128)} fusion(f32[48,1024]{1,0:T(8,128)S(1)} %get-tuple-element.224, f32[48,1024]{1,0:T(8,128)S(1)} %get-tuple-element.228, f32[]{:T(128)} %get-tuple-element.280, f32[1024]{0:T(1024)S(1)} %bitcast.125, f32[1024]{0:T(1024)S(1)} %bitcast.129, f32[1024]{0:T(1024)S(1)} %bitcast.121, f32[1024]{0:T(1024)S(1)} %bitcast.133, ...), kind=kOutput, calls=%fused_computation.6.clone.1.clone | convolution fusion | flops 622854144 | bytes 409616 | tf_op jit(solution)/shard_map/while/body/eval_jaxpr/dot_general | solution.py:38
  70.7 0.7 dynamic_update_slice.27
  71.4 4.1 %multiply_reduce_fusion.6 = f32[]{:T(128)} fusion(f32[]{:T(128)} %get-tuple-element.280, f32[1024]{0:T(1024)S(1)} %bitcast.126, f32[1024]{0:T(1024)S(1)} %bitcast.130, f32[1024]{0:T(1024)S(1)} %bitcast.122, f32[1024]{0:T(1024)S(1)} %bitcast.134, f32[]{:T(128)} %get-tuple-element.277, f32[]{:T(128)} %get-tuple-element.276), kind=kLoop, calls=%fused_computation.7.clone.1.clone | loop fusion | flops 15728639 | bytes 16400 | tf_op jit(solution)/shard_map/while/body/eval_jaxpr/reduce_sum | solution.py:83
  75.5 0.7 dynamic_update_slice.26
  76.2 0.6 dynamic_slice.32
  76.8 0.6 iota_compare_fusion.6
  77.4 3.2 %bitcast_dynamic-update-slice_fusion.6 = (f32[2,48,1024]{2,1,0:T(8,128)S(1)}, f32[48,1024]{1,0:T(8,128)S(1)}) fusion(f32[2,48,1024]{2,1,0:T(8,128)S(1)} %get-tuple-element.258, s32[]{:T(128)} %get-tuple-element.257, f32[]{:T(128)} %get-tuple-element.280, f32[1024]{0:T(1024)S(1)} %bitcast.123, f32[1024]{0:T(1024)S(1)} %bitcast.127, ...), kind=kOutput, calls=%fused_computation.12.clone.1.clone | convolution fusion | flops 115392512 | bytes 510976 | tf_op jit(solution)/shard_map/while/body/eval_jaxpr/dot_general | solution.py:29
  80.5 0.9 select_reduce_fusion.7
  81.5 0.1 copy.15
  82.8 0.6 broadcast_select_fusion.3
  83.4 0.1 fusion.68
  83.4 4.4 %cholesky.73 = f32[48,48]{1,0:T(8,128)S(1)} custom-call(f32[48,48]{1,0:T(8,128)S(1)} %fusion.68), custom_call_target="Cholesky" | custom-call | tf_op jit(solution)/shard_map/while/body/eval_jaxpr/jit(cholesky)/cholesky | solution.py:36
  87.9 0.6 compare_reduce_fusion.3
  88.5 0.6 fusion.69
  89.1 3.7 %custom-call.22 = f32[1,48,48]{1,2,0:T(8,128)S(1)} custom-call(f32[1,48,48]{2,1,0:T(8,128)S(1)} %fusion.69), custom_call_target="InvertDiagBlocksLowerTriangular" | custom-call | tf_op jit(solution)/shard_map/while/body/eval_jaxpr/jit(_cho_solve)/triangular_solve | solution.py:37
  92.7 3.2 %fusion.67 = f32[48,1024]{1,0:T(8,128)S(1)} fusion(f32[]{:T(128)} %get-tuple-element.280, f32[1024]{0:T(1024)S(1)} %bitcast.124, f32[1024]{0:T(1024)S(1)} %bitcast.128, f32[1024]{0:T(1024)S(1)} %bitcast.120, f32[1024]{0:T(1024)S(1)} %bitcast.132, f32[]{:T(128)} %get-tuple-element.277, f32[]{:T(128)} %get-tuple-element.276, ...), kind=kOutput, calls=%fused_computation.9.clone.1.clone | convolution fusion | flops 115392512 | bytes 409612 | tf_op jit(solution)/shard_map/while/body/eval_jaxpr/dot_general | solution.py:32
  95.9 0.4 fusion.70
  96.3 0.3 bitcast_dynamic-update-slice_fusion.7
  96.6 7.3 %multiply_reduce_fusion.7 = f32[]{:T(128)} fusion(f32[48,1024]{1,0:T(8,128)S(1)} %get-tuple-element.224, f32[48,1024]{1,0:T(8,128)S(1)} %get-tuple-element.228, f32[]{:T(128)} %get-tuple-element.280, f32[1024]{0:T(1024)S(1)} %bitcast.125, f32[1024]{0:T(1024)S(1)} %bitcast.129, f32[1024]{0:T(1024)S(1)} %bitcast.121, f32[1024]{0:T(1024)S(1)} %bitcast.133, ...), kind=kOutput, calls=%fused_computation.6.clone.1.clone | convolution fusion | flops 622854144 | bytes 409616 | tf_op jit(solution)/shard_map/while/body/eval_jaxpr/dot_general | solution.py:38
  104.0 0.7 dynamic_update_slice.27
  104.6 4.1 %multiply_reduce_fusion.6 = f32[]{:T(128)} fusion(f32[]{:T(128)} %get-tuple-element.280, f32[1024]{0:T(1024)S(1)} %bitcast.126, f32[1024]{0:T(1024)S(1)} %bitcast.130, f32[1024]{0:T(1024)S(1)} %bitcast.122, f32[1024]{0:T(1024)S(1)} %bitcast.134, f32[]{:T(128)} %get-tuple-element.277, f32[]{:T(128)} %get-tuple-element.276), kind=kLoop, calls=%fused_computation.7.clone.1.clone | loop fusion | flops 15728639 | bytes 16400 | tf_op jit(solution)/shard_map/while/body/eval_jaxpr/reduce_sum | solution.py:83
  108.8 0.7 dynamic_update_slice.26
  109.4 0.6 fusion.22
  110.0 39.8 %psum.15 = s32[1]{0:T(128)} all-reduce(s32[1]{0:T(128)} %bitcast.25), channel_id=1, replica_groups=mesh['prow'=4,'pcol'=8] {'prow','pcol'}, use_global_device_ids=true, to_apply=%region_10.11 | all-reduce | flops 1 | bytes 8 | tf_op jit(solution)/shard_map/psum | solution.py:68
  149.8 41.3 %psum.14 = f32[]{:T(128)} all-reduce(f32[]{:T(128)} %fusion.22), channel_id=1, replica_groups=mesh['prow'=4,'pcol'=8] {'prow','pcol'}, use_global_device_ids=true, to_apply=%region_8.9 | all-reduce | flops 1 | bytes 8 | tf_op jit(solution)/shard_map/psum | solution.py:94
  191.9 0.5 fusion.25
  192.4 1.0 select_bitcast_fusion
  (32 shorter events, 0.3 us)
Async XLA Ops:
  0.6 41.4 %copy-start = (bf16[1,48,1024]{2,1,0:T(8,128)(2,1)S(1)}, bf16[1,48,1024]{2,1,0:T(8,128)(2,1)}, u32[]{:S(2)}) copy-start(bf16[1,48,1024]{2,1,0:T(8,128)(2,1)} %param.11) | copy-start | bytes 294916
  0.6 5.9 %collective-permute-start = (bf16[1,48,1024]{2,1,0:T(8,128)(2,1)}, bf16[1,48,1024]{2,1,0:T(8,128)(2,1)S(1)}, u32[]{:S(2)}, u32[]{:S(2)}) collective-permute-start(bf16[1,48,1024]{2,1,0:T(8,128)(2,1)} %param.11), channel_id=1, source_target_pairs={{0,1},{1,2},{2,3},{3,4},{4,5},{5,6},{6,7},{7,0},{8,9},{9,10},{10,1... | collective-permute-start | bytes 294920 | tf_op jit(solution)/shard_map/ppermute | solution.py:71
  6.6 10.7 %collective-permute-start.1 = (bf16[1,48,1024]{2,1,0:T(8,128)(2,1)S(1)}, bf16[1,48,1024]{2,1,0:T(8,128)(2,1)S(1)}, u32[]{:S(2)}, u32[]{:S(2)}) collective-permute-start(bf16[1,48,1024]{2,1,0:T(8,128)(2,1)S(1)} %collective-permute-done), channel_id=1, source_target_pairs={{0,1},{1,2},{2,3},{3,4},{4,5},{5,6},{6,7},{7,0},{8,9},{9,10},{10,1... | collective-permute-start | bytes 294920 | tf_op jit(solution)/shard_map/ppermute | solution.py:71
  17.2 4.9 %collective-permute-start.2 = (bf16[1,48,1024]{2,1,0:T(8,128)(2,1)S(1)}, bf16[1,48,1024]{2,1,0:T(8,128)(2,1)S(1)}, u32[]{:S(2)}, u32[]{:S(2)}) collective-permute-start(bf16[1,48,1024]{2,1,0:T(8,128)(2,1)S(1)} %collective-permute-done.1), channel_id=1, source_target_pairs={{0,1},{1,2},{2,3},{3,4},{4,5},{5,6},{6,7},{7,0},{8,9},{9,10},{10,1... | collective-permute-start | bytes 294920 | tf_op jit(solution)/shard_map/ppermute | solution.py:71
  22.2 4.9 %collective-permute-start.3 = (bf16[1,48,1024]{2,1,0:T(8,128)(2,1)S(1)}, bf16[1,48,1024]{2,1,0:T(8,128)(2,1)S(1)}, u32[]{:S(2)}, u32[]{:S(2)}) collective-permute-start(bf16[1,48,1024]{2,1,0:T(8,128)(2,1)S(1)} %collective-permute-done.2), channel_id=1, source_target_pairs={{0,1},{1,2},{2,3},{3,4},{4,5},{5,6},{6,7},{7,0},{8,9},{9,10},{10,1... | collective-permute-start | bytes 294920 | tf_op jit(solution)/shard_map/ppermute | solution.py:71
  27.1 4.9 %collective-permute-start.4 = (bf16[1,48,1024]{2,1,0:T(8,128)(2,1)S(1)}, bf16[1,48,1024]{2,1,0:T(8,128)(2,1)S(1)}, u32[]{:S(2)}, u32[]{:S(2)}) collective-permute-start(bf16[1,48,1024]{2,1,0:T(8,128)(2,1)S(1)} %collective-permute-done.3), channel_id=1, source_target_pairs={{0,1},{1,2},{2,3},{3,4},{4,5},{5,6},{6,7},{7,0},{8,9},{9,10},{10,1... | collective-permute-start | bytes 294920 | tf_op jit(solution)/shard_map/ppermute | solution.py:71
  32.1 4.9 %collective-permute-start.5 = (bf16[1,48,1024]{2,1,0:T(8,128)(2,1)S(1)}, bf16[1,48,1024]{2,1,0:T(8,128)(2,1)S(1)}, u32[]{:S(2)}, u32[]{:S(2)}) collective-permute-start(bf16[1,48,1024]{2,1,0:T(8,128)(2,1)S(1)} %collective-permute-done.4), channel_id=1, source_target_pairs={{0,1},{1,2},{2,3},{3,4},{4,5},{5,6},{6,7},{7,0},{8,9},{9,10},{10,1... | collective-permute-start | bytes 294920 | tf_op jit(solution)/shard_map/ppermute | solution.py:71
  37.0 4.9 %collective-permute-start.6 = (bf16[1,48,1024]{2,1,0:T(8,128)(2,1)S(1)}, bf16[1,48,1024]{2,1,0:T(8,128)(2,1)S(1)}, u32[]{:S(2)}, u32[]{:S(2)}) collective-permute-start(bf16[1,48,1024]{2,1,0:T(8,128)(2,1)S(1)} %collective-permute-done.5), channel_id=1, source_target_pairs={{0,1},{1,2},{2,3},{3,4},{4,5},{5,6},{6,7},{7,0},{8,9},{9,10},{10,1... | collective-permute-start | bytes 294920 | tf_op jit(solution)/shard_map/ppermute | solution.py:71
  42.2 0.8 copy-start.1
